TPU v7x, 512 devices: a whole 4x4x16 slice. The times are simulated.
512 devices in a mesh: depth: 32 (over y, x, core), tile: 16 (over z).
Axes of the slice: x: 4, y: 4, z: 16, core: 2. Of those that a mesh axis runs over, the one named last changes fastest.
Arguments:
- field: float32 [128, 1536, 1024], P('depth', 'tile'), may hold values from -6 to 6
Outputs:
- image: float32 [4, 1536, 1024], P(None, ('tile', 'depth'))
All inputs are finite; a program needn't handle non-finite values.
Results may differ from a plain program's by a relative error of at most 0.0003.
Values sent between devices are 32-bit elements; how exact they have to be, the bound alone decides.
No kernel may reach another device: no remote copies, remote signals or barrier semaphores. Data moves between devices by JAX's collectives and lax.ppermute only.
A program may use at most 64 MiB of HBM per device.

v0:
```python
import jax
import jax.numpy as jnp
from jax import lax
from jax.sharding import PartitionSpec as P

centres = (-1.2, 0.3, 1.5)
spreads = (0.25, 0.35, 0.3)
heights = (2.0, 1.0, 3.0)
floor_density = 0.05
light_cols = 0.48
light_rows = 0.6
light_depth = 0.64


def from_behind(block, axis, distance):
    devices = range(lax.axis_size(axis))
    route = [(i - distance, i) for i in devices if i - distance in devices]
    return lax.ppermute(block, axis, route)


def extended(cells, sides, width):
    for axis, dim in sides:
        count = lax.axis_size(axis)
        ends = count - 1
        head = lax.slice_in_dim(cells, 0, width, axis=dim)
        tail = lax.slice_in_dim(cells, cells.shape[dim] - width, cells.shape[dim], axis=dim)
        cells = jnp.concatenate(
            [
                lax.ppermute(tail, axis, [(i, (i + 1) % count) for i in range(ends)]),
                cells,
                lax.ppermute(head, axis, [((i + 1) % count, i) for i in range(ends)]),
            ],
            axis=dim,
        )
    return cells


def emission(sample, slope_cols, slope_rows, slope_depth):
    density = floor_density + jnp.zeros_like(sample)
    for centre, spread, bump_height in zip(centres, spreads, heights):
        scaled = (sample - centre) / spread
        density = density + bump_height * jnp.exp(-scaled * scaled)
    facing = light_cols * slope_cols + light_rows * slope_rows + light_depth * slope_depth
    length = slope_cols * slope_cols + slope_rows * slope_rows + slope_depth * slope_depth + 1.0
    shading = 0.3 + 0.7 * jnp.abs(facing) * lax.rsqrt(length)
    colour = jnp.stack(
        [
            shading * jax.nn.sigmoid(2.0 * sample),
            shading * jnp.exp(-sample * sample),
            shading * jax.nn.sigmoid(-2.0 * sample),
        ]
    )
    return (density, colour)


def integrate(density, colour, spacing):
    optics = spacing * density
    running = jnp.cumsum(optics, axis=0)
    before = jnp.concatenate([jnp.zeros_like(optics[:1]), running[:-1]], axis=0)
    weight = jnp.exp(-before) * -jnp.expm1(-optics)
    return (jnp.sum(weight[None] * colour, axis=1), jnp.exp(-running[-1]))


def blend_all(pieces):
    colour_in, through_in = pieces
    passed = jnp.cumprod(through_in, axis=1)
    before = jnp.concatenate([jnp.ones_like(through_in[:, :1]), passed[:, :-1]], axis=1)
    return (jnp.sum(before * colour_in, axis=1), passed[:, -1])


def local(field):
    planes, row_count, col_count = field.shape
    depth_count = lax.axis_size("depth")
    spacing = 3.0 / (planes * depth_count)
    following = from_behind(field[:1], "depth", -1)
    further = jnp.concatenate([field[1:], following], axis=0)
    sample = 0.5 * (field + further)
    slope_depth = further - field
    edge_rows = jnp.concatenate([sample[:, :1], sample[:, -1:]], axis=1)
    edge_padded = extended(edge_rows, (("tile", 1),), 1)
    padded = jnp.concatenate([edge_padded[:, :1], sample, edge_padded[:, -1:]], axis=1)
    slope_rows = 0.5 * (padded[:, 2:] - padded[:, :-2])
    zero_col = jnp.zeros_like(sample[..., :1])
    slope_cols = 0.5 * (
        jnp.concatenate([sample[..., 1:], zero_col], axis=-1)
        - jnp.concatenate([zero_col, sample[..., :-1]], axis=-1)
    )
    density, colour = emission(sample, slope_cols, slope_rows, slope_depth)
    colour_sum, through = integrate(density, colour, spacing)
    row_share = row_count // depth_count
    colour_parts = colour_sum.reshape(3, depth_count, row_share, col_count)
    through_parts = through.reshape(1, depth_count, row_share, col_count)
    colour_out, through_out = blend_all(
        (
            lax.all_to_all(colour_parts, "depth", split_axis=1, concat_axis=1, tiled=True),
            lax.all_to_all(through_parts, "depth", split_axis=1, concat_axis=1, tiled=True),
        )
    )
    return jnp.concatenate([colour_out, 1.0 - through_out], axis=0)


def solution(mesh):
    return jax.shard_map(
        local,
        mesh=mesh,
        in_specs=(P("depth", "tile", None),),
        out_specs=P(None, ("tile", "depth"), None),
        check_vma=False,
    )
```

profile of v0, /device:TPU:96, one launch (start us, length us, event | category | flops | bytes accessed | tf_op | source)
XLA Modules:
  0.0 78.3 jit_solution(17771362351667191256)
XLA Ops:
  0.0 1.1 %slice.39 = f32[1,96,1024]{2,1,0:T(8,128)S(1)} slice(f32[4,96,1024]{2,1,0:T(8,128)} %param.1), slice={[0:1], [0:96], [0:1024]} | slice | bytes 786432 | tf_op jit(solution)/shard_map/slice | solution.py:75
  1.1 1.3 %collective-permute-start = (f32[1,96,1024]{2,1,0:T(8,128)S(1)}, f32[1,96,1024]{2,1,0:T(8,128)S(1)}, u32[]{:S(2)}, u32[]{:S(2)}) collective-permute-start(f32[1,96,1024]{2,1,0:T(8,128)S(1)} %slice.39), channel_id=1, source_target_pairs={{16,0},{32,16},{48,32},{64,48},{80,64},{96,80},{112,96},{128,112},... | collective-permute-start | bytes 1179656 | tf_op jit(solution)/shard_map/ppermute | solution.py:18
  2.4 1.4 %slice.38 = f32[3,96,1024]{2,1,0:T(8,128)S(1)} slice(f32[4,96,1024]{2,1,0:T(8,128)} %param.1), slice={[1:4], [0:96], [0:1024]} | slice | bytes 2359296 | tf_op jit(solution)/shard_map/slice | solution.py:76
  3.8 0.0 copy-start.1
  3.8 1.0 %collective-permute-done = f32[1,96,1024]{2,1,0:T(8,128)S(1)} collective-permute-done((f32[1,96,1024]{2,1,0:T(8,128)S(1)}, f32[1,96,1024]{2,1,0:T(8,128)S(1)}, u32[]{:S(2)}, u32[]{:S(2)}) %collective-permute-start) | collective-permute-done | bytes 393248 | tf_op jit(solution)/shard_map/ppermute | solution.py:18
  4.8 0.0 copy-done
  4.8 0.3 broadcast_multiply_fusion
  5.1 0.0 copy-done.1
  5.1 2.3 %fusion.22 = (f32[4,96,1023]{2,1,0:T(8,128)}, f32[4,96,1023]{2,1,0:T(8,128)}) fusion(f32[4,96,1024]{2,1,0:T(8,128)S(1)} %get-tuple-element.7), kind=kLoop, calls=%fused_computation.38 | loop fusion | bytes 6285312 | tf_op jit(solution)/shard_map/slice | solution.py:85
  7.4 0.6 fusion.23
  8.0 2.0 %collective-permute-start.1 = (f32[4,1,1024]{2,1,0:T(1,128)}, f32[4,1,1024]{2,1,0:T(1,128)S(1)}, u32[]{:S(2)}, u32[]{:S(2)}) collective-permute-start(f32[4,1,1024]{2,1,0:T(1,128)} %get-tuple-element.14), channel_id=1, source_target_pairs={{1,0},{2,1},{3,2},{4,3},{5,4},{6,5},{7,6},{8,7},{9,8},{10,9},{11,1... | collective-permute-start | bytes 49160 | tf_op jit(solution)/shard_map/ppermute | solution.py:31
  10.0 5.0 %collective-permute-start.2 = (f32[4,1,1024]{2,1,0:T(1,128)}, f32[4,1,1024]{2,1,0:T(1,128)}, u32[]{:S(2)}, u32[]{:S(2)}) collective-permute-start(f32[4,1,1024]{2,1,0:T(1,128)} %get-tuple-element.15), channel_id=1, source_target_pairs={{0,1},{1,2},{2,3},{3,4},{4,5},{5,6},{6,7},{7,8},{8,9},{9,10},{10,1... | collective-permute-start | bytes 49160 | tf_op jit(solution)/shard_map/ppermute | solution.py:29
  15.1 1.5 %fusion.19 = f32[4,96,1024]{2,1,0:T(8,128)S(1)} fusion(f32[4,96,1024]{2,1,0:T(8,128)S(1)} %get-tuple-element.8), kind=kOutput, calls=%fused_computation.37 | output fusion | flops 8650752 | bytes 3145728 | tf_op jit(solution)/shard_map/jit(cumsum)/reduce_window_sum | solution.py:58
  16.6 0.8 %fusion.17 = f32[1,96,1024]{2,1,0:T(8,128)} fusion(f32[4,96,1024]{2,1,0:T(8,128)S(1)} %fusion.19), kind=kLoop, calls=%fused_computation.33 | loop fusion | flops 98304 | bytes 786432 | tf_op jit(solution)/shard_map/exp | solution.py:61
  17.4 1.1 %slice.52 = f32[3,96,1024]{2,1,0:T(8,128)} slice(f32[4,96,1024]{2,1,0:T(8,128)S(1)} %fusion.19), slice={[0:3], [0:96], [0:1024]} | slice | bytes 2359296 | tf_op jit(solution)/shard_map/slice | solution.py:59
  18.5 2.2 %exp.38 = f32[1,32,3,1024]{3,0,2,1:T(1,128)} reshape(f32[1,96,1024]{2,1,0:T(8,128)} %fusion.17) | data formatting | bytes 786432 | tf_op jit(solution)/shard_map/exp | solution.py:61
  20.7 13.8 %all-to-all-start = ((f32[1,32,3,1024]{3,0,2,1:T(1,128)}), f32[1,32,3,1024]{3,0,2,1:T(1,128)}, u32[]{:S(2)}, u32[]{:S(2)}) async-start(f32[1,32,3,1024]{3,0,2,1:T(1,128)} %exp.38), calls=%async_computation | async-start | bytes 786432 | tf_op jit(solution)/shard_map/all_to_all | solution.py:96
  34.5 0.0 collective-permute-done.1
  34.5 0.0 collective-permute-done.2
  34.6 4.0 %multiply_bitcast_fusion.1 = (f32[1,4,96,1024]{3,2,1,0:T(8,128)S(1)}, f32[4,96,1024]{2,1,0:T(8,128)S(1)}) fusion(f32[4,96,1024]{2,1,0:T(8,128)S(1)} %get-tuple-element.8, f32[4,96,1024]{2,1,0:T(8,128)} %param.1, f32[1,96,1024]{2,1,0:T(8,128)S(1)} %collective-permute-done, f32[3,96,1024]{2,1,0:T(8,128)} %copy-done.1, f32[4,96,1024]{2,1,0:T(8,128)S(1)} %get-tuple-element.7, ...), kind=kLoop, calls=%fused_computation.24 | loop fusion | flops 10616832 | bytes 12612608 | tf_op jit(solution)/shard_map/stack | solution.py:46
  38.5 2.4 %fusion.12 = (f32[1,4,96,1024]{3,2,1,0:T(8,128)S(1)}, f32[1,4,96,1024]{3,2,1,0:T(8,128)S(1)}, f32[4,96,1024]{2,1,0:T(8,128)S(1)}) fusion(f32[4,96,1024]{2,1,0:T(8,128)S(1)} %get-tuple-element.6, f32[4,96,1024]{2,1,0:T(8,128)S(1)} %get-tuple-element.8, f32[3,96,1024]{2,1,0:T(8,128)S(1)} %copy-done.2), kind=kLoop, calls=%fused_computation.17 | loop fusion | flops 12189696 | bytes 9043968 | tf_op jit(solution)/shard_map/stack | solution.py:46
  40.9 1.9 %fusion = f32[3,96,1024]{2,1,0:T(8,128)} fusion(f32[1,4,96,1024]{3,2,1,0:T(8,128)S(1)} %get-tuple-element.10, f32[1,4,96,1024]{3,2,1,0:T(8,128)S(1)} %get-tuple-element.9, f32[1,4,96,1024]{3,2,1,0:T(8,128)S(1)} %get-tuple-element.5, f32[4,96,1024]{2,1,0:T(8,128)S(1)} %get-tuple-element.11), kind=kLoop, calls=%fused_computation.1 | loop fusion | flops 4423680 | bytes 7471104 | tf_op jit(solution)/shard_map/reduce_sum | solution.py:61
  42.8 1.6 %reshape.34 = f32[3,32,3,1024]{3,2,1,0:T(4,128)S(1)} reshape(f32[3,96,1024]{2,1,0:T(8,128)} %fusion) | data formatting | bytes 2359296 | tf_op jit(solution)/shard_map/reshape | solution.py:91
  44.4 1.5 %copy.6 = f32[3,32,3,1024]{3,2,0,1:T(4,128)} copy(f32[3,32,3,1024]{3,2,1,0:T(4,128)S(1)} %reshape.34) | data formatting | bytes 2359296 | tf_op jit(solution)/shard_map/reshape | solution.py:91
  45.8 0.0 all-to-all-done
  45.8 7.3 %all-to-all-start.1 = ((f32[3,32,3,1024]{3,2,0,1:T(4,128)}), f32[3,32,3,1024]{3,2,0,1:T(4,128)S(1)}, u32[]{:S(2)}, u32[]{:S(2)}) async-start(f32[3,32,3,1024]{3,2,0,1:T(4,128)} %copy.6), calls=%async_computation.1 | async-start | bytes 3145728 | tf_op jit(solution)/shard_map/all_to_all | solution.py:95
  53.2 1.1 %fusion.15 = f32[1,32,3,1024]{3,2,1,0:T(4,128)S(1)} fusion(f32[1,32,3,1024]{3,0,2,1:T(1,128)} %all-to-all-done), kind=kOutput, calls=%fused_computation.29 | output fusion | flops 3047424 | bytes 786432 | tf_op jit(solution)/shard_map/jit(cumprod)/reduce_window | solution.py:66
  54.3 0.1 slice.51
  54.4 0.1 pad_bitcast_fusion
  54.6 22.5 %all-to-all-done.1 = f32[3,32,3,1024]{3,2,0,1:T(4,128)S(1)} async-done(((f32[3,32,3,1024]{3,2,0,1:T(4,128)}), f32[3,32,3,1024]{3,2,0,1:T(4,128)S(1)}, u32[]{:S(2)}, u32[]{:S(2)}) %all-to-all-start.1) | async-done | bytes 1179680 | tf_op jit(solution)/shard_map/all_to_all | solution.py:95
  77.1 0.5 multiply_reduce_fusion
  77.6 0.7 copy.8
  (5 shorter events, 0.0 us)
Async XLA Ops:
  0.0 4.8 %copy-start = (f32[4,96,1024]{2,1,0:T(8,128)S(1)}, f32[4,96,1024]{2,1,0:T(8,128)}, u32[]{:S(2)}) copy-start(f32[4,96,1024]{2,1,0:T(8,128)} %param.1) | copy-start | bytes 4718596
  1.1 3.6 %collective-permute-start = (f32[1,96,1024]{2,1,0:T(8,128)S(1)}, f32[1,96,1024]{2,1,0:T(8,128)S(1)}, u32[]{:S(2)}, u32[]{:S(2)}) collective-permute-start(f32[1,96,1024]{2,1,0:T(8,128)S(1)} %slice.39), channel_id=1, source_target_pairs={{16,0},{32,16},{48,32},{64,48},{80,64},{96,80},{112,96},{128,112},... | collective-permute-start | bytes 1179656 | tf_op jit(solution)/shard_map/ppermute | solution.py:18
  3.8 1.3 %copy-start.1 = (f32[3,96,1024]{2,1,0:T(8,128)}, f32[3,96,1024]{2,1,0:T(8,128)S(1)}, u32[]{:S(2)}) copy-start(f32[3,96,1024]{2,1,0:T(8,128)S(1)} %slice.38) | copy-start | bytes 3538948
  8.0 26.5 %collective-permute-start.1 = (f32[4,1,1024]{2,1,0:T(1,128)}, f32[4,1,1024]{2,1,0:T(1,128)S(1)}, u32[]{:S(2)}, u32[]{:S(2)}) collective-permute-start(f32[4,1,1024]{2,1,0:T(1,128)} %get-tuple-element.14), channel_id=1, source_target_pairs={{1,0},{2,1},{3,2},{4,3},{5,4},{6,5},{7,6},{8,7},{9,8},{10,9},{11,1... | collective-permute-start | bytes 49160 | tf_op jit(solution)/shard_map/ppermute | solution.py:31
  10.0 24.5 %collective-permute-start.2 = (f32[4,1,1024]{2,1,0:T(1,128)}, f32[4,1,1024]{2,1,0:T(1,128)}, u32[]{:S(2)}, u32[]{:S(2)}) collective-permute-start(f32[4,1,1024]{2,1,0:T(1,128)} %get-tuple-element.15), channel_id=1, source_target_pairs={{0,1},{1,2},{2,3},{3,4},{4,5},{5,6},{6,7},{7,8},{8,9},{9,10},{10,1... | collective-permute-start | bytes 49160 | tf_op jit(solution)/shard_map/ppermute | solution.py:29
  20.7 25.1 %all-to-all-start = ((f32[1,32,3,1024]{3,0,2,1:T(1,128)}), f32[1,32,3,1024]{3,0,2,1:T(1,128)}, u32[]{:S(2)}, u32[]{:S(2)}) async-start(f32[1,32,3,1024]{3,0,2,1:T(1,128)} %exp.38), calls=%async_computation | async-start | bytes 786432 | tf_op jit(solution)/shard_map/all_to_all | solution.py:96
  34.6 4.0 %copy-start.2 = (f32[3,96,1024]{2,1,0:T(8,128)S(1)}, f32[3,96,1024]{2,1,0:T(8,128)}, u32[]{:S(2)}) copy-start(f32[3,96,1024]{2,1,0:T(8,128)} %slice.52) | copy-start | bytes 3538948
  45.8 31.2 %all-to-all-start.1 = ((f32[3,32,3,1024]{3,2,0,1:T(4,128)}), f32[3,32,3,1024]{3,2,0,1:T(4,128)S(1)}, u32[]{:S(2)}, u32[]{:S(2)}) async-start(f32[3,32,3,1024]{3,2,0,1:T(4,128)} %copy.6), calls=%async_computation.1 | async-start | bytes 3145728 | tf_op jit(solution)/shard_map/all_to_all | solution.py:95
where the time goes:
time: 78.7 us; the launch traced here: 78.3 us
  starting transfers between devices  29.5 us (37%)
  waiting for transfers between devices  23.5 us (30%)
  local copies, waits for them, and re-layouts  12.6 us (16%)
  other arithmetic  12.5 us (16%)
    all_to_all x1, waiting for transfers between devices, local(): lax.all_to_all(colour_parts, 'depth', split_axis=1, concat_axis=1, tiled=...  22.5 us
    all_to_all x1, starting transfers between devices, local(): lax.all_to_all(through_parts, 'depth', split_axis=1, concat_axis=1, tiled...  13.8 us
    all_to_all x1, starting transfers between devices, local(): lax.all_to_all(colour_parts, 'depth', split_axis=1, concat_axis=1, tiled=...  7.32 us
    another operation x2, other arithmetic, emission(): jnp.stack([shading * jax.nn.sigmoid(2.0 * sample), shading * jnp.exp(-sam...  6.33 us
    ppermute x1, starting transfers between devices, extended(): lax.ppermute(tail, axis, [(i, (i + 1) % count) for i in range(ends)])  5.04 us
    reshape x2, local copies, waits for them, and re-layouts, local(): colour_parts = colour_sum.reshape(3, depth_count, row_share, col_count)  3.05 us
    slice x1, local copies, waits for them, and re-layouts, local(): sample[..., 1:]  2.26 us
    exp x1, local copies, waits for them, and re-layouts, integrate(): return (jnp.sum(weight[None] * colour, axis=1), jnp.exp(-running[-1]))  2.22 us
  transfers between devices with their start and end apart: 5, of which 2 were waited for; matrix products, arithmetic and copies ran while one was open for 25% of the time, Pallas kernels for 0%

commit v1 on v0

--- a/solution.py
+++ b/solution.py
@@ -10,6 +10,18 @@
 light_cols = 0.48
 light_rows = 0.6
 light_depth = 0.64
+
+
+def play_series(body, peer_axis):
+    return jnp.concatenate(
+        lax.all_to_all(
+            jnp.stack(jnp.split(body, lax.axis_size(peer_axis), axis=1)),
+            axis_name=peer_axis,
+            split_axis=0,
+            concat_axis=0,
+        ),
+        axis=1,
+    )
 
 
 def from_behind(block, axis, distance):
@@ -92,7 +104,7 @@
     through_parts = through.reshape(1, depth_count, row_share, col_count)
     colour_out, through_out = blend_all(
         (
-            lax.all_to_all(colour_parts, "depth", split_axis=1, concat_axis=1, tiled=True),
+            play_series(colour_parts, "depth"),
             lax.all_to_all(through_parts, "depth", split_axis=1, concat_axis=1, tiled=True),
         )
     )

time: 78.7 us -> 73.3 us (0.931)
  the two profiles are of different devices: /device:TPU:96 before, /device:TPU:1 now
where the time goes in v1:
time: 73.3 us; the launch traced here: 72.8 us
  starting transfers between devices  30.4 us (41%)
  waiting for transfers between devices  16.9 us (23%)
  local copies, waits for them, and re-layouts  13.7 us (19%)
  other arithmetic  11.4 us (16%)
    all_to_all x1, waiting for transfers between devices, play_series(): lax.all_to_all(jnp.stack(jnp.split(body, lax.axis_size(peer_axis), axis=1...  16.9 us
    ppermute x1, starting transfers between devices, from_behind(): return lax.ppermute(block, axis, route)  8.75 us
    all_to_all x1, starting transfers between devices, local(): lax.all_to_all(through_parts, 'depth', split_axis=1, concat_axis=1, tiled...  8.41 us
    all_to_all x1, starting transfers between devices, play_series(): lax.all_to_all(jnp.stack(jnp.split(body, lax.axis_size(peer_axis), axis=1...  7.38 us
    another operation x2, other arithmetic, emission(): jnp.stack([shading * jax.nn.sigmoid(2.0 * sample), shading * jnp.exp(-sam...  6.33 us
    ppermute x1, starting transfers between devices, extended(): lax.ppermute(tail, axis, [(i, (i + 1) % count) for i in range(ends)])  4.58 us
    another operation x2, local copies, waits for them, and re-layouts, play_series(): jnp.stack(jnp.split(body, lax.axis_size(peer_axis), axis=1))  2.25 us
    slice x1, local copies, waits for them, and re-layouts, local(): sample[..., 1:]  2.22 us
  transfers between devices with their start and end apart: 5, of which 1 were waited for; matrix products, arithmetic and copies ran while one was open for 26% of the time, Pallas kernels for 0%

profile of v1, /device:TPU:1, one launch (start us, length us, event | category | flops | bytes accessed | tf_op | source)
XLA Modules:
  0.0 72.8 jit_solution(812944307918909386)
XLA Ops:
  0.0 1.1 %slice.39 = f32[1,96,1024]{2,1,0:T(8,128)S(1)} slice(f32[4,96,1024]{2,1,0:T(8,128)} %param.1), slice={[0:1], [0:96], [0:1024]} | slice | bytes 786432 | tf_op jit(solution)/shard_map/slice | solution.py:87
  1.1 8.7 %collective-permute-start = (f32[1,96,1024]{2,1,0:T(8,128)S(1)}, f32[1,96,1024]{2,1,0:T(8,128)S(1)}, u32[]{:S(2)}, u32[]{:S(2)}) collective-permute-start(f32[1,96,1024]{2,1,0:T(8,128)S(1)} %slice.39), channel_id=1, source_target_pairs={{16,0},{32,16},{48,32},{64,48},{80,64},{96,80},{112,96},{128,112},... | collective-permute-start | bytes 1179656 | tf_op jit(solution)/shard_map/ppermute | solution.py:30
  9.9 1.4 %slice.38 = f32[3,96,1024]{2,1,0:T(8,128)S(1)} slice(f32[4,96,1024]{2,1,0:T(8,128)} %param.1), slice={[1:4], [0:96], [0:1024]} | slice | bytes 2359296 | tf_op jit(solution)/shard_map/slice | solution.py:88
  11.3 0.0 copy-start.1
  11.3 0.0 collective-permute-done
  11.3 0.4 broadcast_multiply_fusion
  11.6 0.7 copy-done.1
  12.3 2.2 %fusion.23 = (f32[4,96,1023]{2,1,0:T(8,128)}, f32[4,96,1023]{2,1,0:T(8,128)}) fusion(f32[4,96,1024]{2,1,0:T(8,128)S(1)} %get-tuple-element.7), kind=kLoop, calls=%fused_computation.103 | loop fusion | bytes 6285312 | tf_op jit(solution)/shard_map/slice | solution.py:97
  14.5 0.6 fusion.24
  15.2 1.3 %collective-permute-start.1 = (f32[4,1,1024]{2,1,0:T(1,128)}, f32[4,1,1024]{2,1,0:T(1,128)S(1)}, u32[]{:S(2)}, u32[]{:S(2)}) collective-permute-start(f32[4,1,1024]{2,1,0:T(1,128)} %get-tuple-element.14), channel_id=1, source_target_pairs={{1,0},{2,1},{3,2},{4,3},{5,4},{6,5},{7,6},{8,7},{9,8},{10,9},{11,1... | collective-permute-start | bytes 49160 | tf_op jit(solution)/shard_map/ppermute | solution.py:43
  16.4 4.6 %collective-permute-start.2 = (f32[4,1,1024]{2,1,0:T(1,128)}, f32[4,1,1024]{2,1,0:T(1,128)}, u32[]{:S(2)}, u32[]{:S(2)}) collective-permute-start(f32[4,1,1024]{2,1,0:T(1,128)} %get-tuple-element.15), channel_id=1, source_target_pairs={{0,1},{1,2},{2,3},{3,4},{4,5},{5,6},{6,7},{7,8},{8,9},{9,10},{10,1... | collective-permute-start | bytes 49160 | tf_op jit(solution)/shard_map/ppermute | solution.py:41
  21.0 1.5 %fusion.20 = f32[4,96,1024]{2,1,0:T(8,128)S(1)} fusion(f32[4,96,1024]{2,1,0:T(8,128)S(1)} %get-tuple-element.8), kind=kOutput, calls=%fused_computation.102 | output fusion | flops 8650752 | bytes 3145728 | tf_op jit(solution)/shard_map/jit(cumsum)/reduce_window_sum | solution.py:70
  22.5 0.8 %fusion.18 = f32[1,96,1024]{2,1,0:T(8,128)} fusion(f32[4,96,1024]{2,1,0:T(8,128)S(1)} %fusion.20), kind=kLoop, calls=%fused_computation.34 | loop fusion | flops 98304 | bytes 786432 | tf_op jit(solution)/shard_map/exp | solution.py:73
  23.3 1.1 %slice.52 = f32[3,96,1024]{2,1,0:T(8,128)} slice(f32[4,96,1024]{2,1,0:T(8,128)S(1)} %fusion.20), slice={[0:3], [0:96], [0:1024]} | slice | bytes 2359296 | tf_op jit(solution)/shard_map/slice | solution.py:71
  24.4 2.2 %exp.38 = f32[1,32,3,1024]{3,0,2,1:T(1,128)} reshape(f32[1,96,1024]{2,1,0:T(8,128)} %fusion.18) | data formatting | bytes 786432 | tf_op jit(solution)/shard_map/exp | solution.py:73
  26.6 8.4 %all-to-all-start = ((f32[1,32,3,1024]{3,0,2,1:T(1,128)}), f32[1,32,3,1024]{3,0,2,1:T(1,128)}, u32[]{:S(2)}, u32[]{:S(2)}) async-start(f32[1,32,3,1024]{3,0,2,1:T(1,128)} %exp.38), calls=%async_computation | async-start | bytes 786432 | tf_op jit(solution)/shard_map/all_to_all | solution.py:108
  35.0 0.0 collective-permute-done.1
  35.1 0.0 collective-permute-done.2
  35.1 4.0 %multiply_bitcast_fusion.1 = (f32[1,4,96,1024]{3,2,1,0:T(8,128)S(1)}, f32[4,96,1024]{2,1,0:T(8,128)S(1)}) fusion(f32[4,96,1024]{2,1,0:T(8,128)S(1)} %get-tuple-element.8, f32[4,96,1024]{2,1,0:T(8,128)} %param.1, f32[1,96,1024]{2,1,0:T(8,128)S(1)} %collective-permute-done, f32[3,96,1024]{2,1,0:T(8,128)} %copy-done.1, f32[4,96,1024]{2,1,0:T(8,128)S(1)} %get-tuple-element.7, ...), kind=kLoop, calls=%fused_computation.23 | loop fusion | flops 10616832 | bytes 12612608 | tf_op jit(solution)/shard_map/stack | solution.py:58
  39.1 2.4 %fusion.12 = (f32[1,4,96,1024]{3,2,1,0:T(8,128)S(1)}, f32[1,4,96,1024]{3,2,1,0:T(8,128)S(1)}, f32[4,96,1024]{2,1,0:T(8,128)S(1)}) fusion(f32[4,96,1024]{2,1,0:T(8,128)S(1)} %get-tuple-element.6, f32[4,96,1024]{2,1,0:T(8,128)S(1)} %get-tuple-element.8, f32[3,96,1024]{2,1,0:T(8,128)S(1)} %copy-done.2), kind=kLoop, calls=%fused_computation.17 | loop fusion | flops 12189696 | bytes 9043968 | tf_op jit(solution)/shard_map/stack | solution.py:58
  41.4 0.8 %fusion = f32[3,96,1024]{2,1,0:T(8,128)S(1)} fusion(f32[1,4,96,1024]{3,2,1,0:T(8,128)S(1)} %get-tuple-element.10, f32[1,4,96,1024]{3,2,1,0:T(8,128)S(1)} %get-tuple-element.9, f32[1,4,96,1024]{3,2,1,0:T(8,128)S(1)} %get-tuple-element.5, f32[4,96,1024]{2,1,0:T(8,128)S(1)} %get-tuple-element.11), kind=kLoop, calls=%fused_computation.1 | loop fusion | flops 4423680 | bytes 7471104 | tf_op jit(solution)/shard_map/reduce_sum | solution.py:73
  42.3 0.5 reshape.40
  43.6 2.2 %copy.134 = f32[32,3,1,3,1024]{4,2,3,1,0:T(1,128)} copy(f32[32,3,1,3,1024]{4,3,1,2,0:T(4,128)S(1)} %constant_dynamic-update-slice_fusion) | data formatting | bytes 2359296 | tf_op jit(solution)/shard_map/stack | solution.py:18
  45.8 0.0 all-to-all-done
  45.8 7.4 %all-to-all-start.1 = ((f32[32,3,1,3,1024]{4,2,3,1,0:T(1,128)}), f32[32,3,1,3,1024]{4,2,3,1,0:T(1,128)S(1)}, u32[]{:S(2)}, u32[]{:S(2)}) async-start(f32[32,3,1,3,1024]{4,2,3,1,0:T(1,128)} %copy.134), calls=%async_computation.1 | async-start | bytes 2359296 | tf_op jit(solution)/shard_map/all_to_all | solution.py:17
  53.2 1.1 %fusion.16 = f32[1,32,3,1024]{3,2,1,0:T(4,128)S(1)} fusion(f32[1,32,3,1024]{3,0,2,1:T(1,128)} %all-to-all-done), kind=kOutput, calls=%fused_computation.30 | output fusion | flops 3047424 | bytes 786432 | tf_op jit(solution)/shard_map/jit(cumprod)/reduce_window | solution.py:78
  54.3 0.1 slice.51
  54.4 0.1 pad_bitcast_fusion
  54.6 0.2 copy.102
  54.8 16.9 %all-to-all-done.1 = f32[32,3,1,3,1024]{4,2,3,1,0:T(1,128)S(1)} async-done(((f32[32,3,1,3,1024]{4,2,3,1,0:T(1,128)}), f32[32,3,1,3,1024]{4,2,3,1,0:T(1,128)S(1)}, u32[]{:S(2)}, u32[]{:S(2)}) %all-to-all-start.1) | async-done | bytes 1179680 | tf_op jit(solution)/shard_map/all_to_all | solution.py:17
  71.7 0.4 fusion.15
  72.1 0.7 copy.137
  (38 shorter events, 0.6 us)
Async XLA Ops:
  0.0 11.3 %copy-start = (f32[4,96,1024]{2,1,0:T(8,128)S(1)}, f32[4,96,1024]{2,1,0:T(8,128)}, u32[]{:S(2)}) copy-start(f32[4,96,1024]{2,1,0:T(8,128)} %param.1) | copy-start | bytes 4718596
  1.1 10.1 %collective-permute-start = (f32[1,96,1024]{2,1,0:T(8,128)S(1)}, f32[1,96,1024]{2,1,0:T(8,128)S(1)}, u32[]{:S(2)}, u32[]{:S(2)}) collective-permute-start(f32[1,96,1024]{2,1,0:T(8,128)S(1)} %slice.39), channel_id=1, source_target_pairs={{16,0},{32,16},{48,32},{64,48},{80,64},{96,80},{112,96},{128,112},... | collective-permute-start | bytes 1179656 | tf_op jit(solution)/shard_map/ppermute | solution.py:30
  11.3 1.0 %copy-start.1 = (f32[3,96,1024]{2,1,0:T(8,128)}, f32[3,96,1024]{2,1,0:T(8,128)S(1)}, u32[]{:S(2)}) copy-start(f32[3,96,1024]{2,1,0:T(8,128)S(1)} %slice.38) | copy-start | bytes 3538948
  15.2 19.9 %collective-permute-start.1 = (f32[4,1,1024]{2,1,0:T(1,128)}, f32[4,1,1024]{2,1,0:T(1,128)S(1)}, u32[]{:S(2)}, u32[]{:S(2)}) collective-permute-start(f32[4,1,1024]{2,1,0:T(1,128)} %get-tuple-element.14), channel_id=1, source_target_pairs={{1,0},{2,1},{3,2},{4,3},{5,4},{6,5},{7,6},{8,7},{9,8},{10,9},{11,1... | collective-permute-start | bytes 49160 | tf_op jit(solution)/shard_map/ppermute | solution.py:43
  16.4 18.6 %collective-permute-start.2 = (f32[4,1,1024]{2,1,0:T(1,128)}, f32[4,1,1024]{2,1,0:T(1,128)}, u32[]{:S(2)}, u32[]{:S(2)}) collective-permute-start(f32[4,1,1024]{2,1,0:T(1,128)} %get-tuple-element.15), channel_id=1, source_target_pairs={{0,1},{1,2},{2,3},{3,4},{4,5},{5,6},{6,7},{7,8},{8,9},{9,10},{10,1... | collective-permute-start | bytes 49160 | tf_op jit(solution)/shard_map/ppermute | solution.py:41
  26.6 19.2 %all-to-all-start = ((f32[1,32,3,1024]{3,0,2,1:T(1,128)}), f32[1,32,3,1024]{3,0,2,1:T(1,128)}, u32[]{:S(2)}, u32[]{:S(2)}) async-start(f32[1,32,3,1024]{3,0,2,1:T(1,128)} %exp.38), calls=%async_computation | async-start | bytes 786432 | tf_op jit(solution)/shard_map/all_to_all | solution.py:108
  35.1 4.0 %copy-start.2 = (f32[3,96,1024]{2,1,0:T(8,128)S(1)}, f32[3,96,1024]{2,1,0:T(8,128)}, u32[]{:S(2)}) copy-start(f32[3,96,1024]{2,1,0:T(8,128)} %slice.52) | copy-start | bytes 3538948
  45.8 25.9 %all-to-all-start.1 = ((f32[32,3,1,3,1024]{4,2,3,1,0:T(1,128)}), f32[32,3,1,3,1024]{4,2,3,1,0:T(1,128)S(1)}, u32[]{:S(2)}, u32[]{:S(2)}) async-start(f32[32,3,1,3,1024]{4,2,3,1,0:T(1,128)} %copy.134), calls=%async_computation.1 | async-start | bytes 2359296 | tf_op jit(solution)/shard_map/all_to_all | solution.py:17
